TPU v7x, 32 devices: a whole 2x2x4 slice. The times are simulated.
32 devices in a mesh: row: 8 (over y, x, core), col: 4 (over z).
Axes of the slice: x: 2, y: 2, z: 4, core: 2. Of those that a mesh axis runs over, the one named last changes fastest.
Arguments:
- row_cells: int32 [3, 8192], P(None, 'row'), may hold values from 0 to 63
- col_cells: int32 [3, 32768], P(None, 'col'), may hold values from 0 to 63
- omega: float32 [16, 32768], P(None, 'col'), may hold values from -6 to 6
Outputs:
- basis: float32 [16, 8192], P(None, 'row')
- image: float32 [16, 32768], P(None, 'col')
- core: float32 [16, 16], replicated
All inputs are finite; a program needn't handle non-finite values.
Results may differ from a plain program's by a relative error of at most 0.0001.
Values sent between devices are 32-bit elements; how exact they have to be, the bound alone decides.
A program may use at most 64 MiB of HBM per device.

v0:
```python
import jax
import jax.numpy as jnp
from jax import lax
from jax.sharding import PartitionSpec as P


def kernel_tile(rows, cols):
    first = (rows[0][:, None] - cols[0][None, :]).astype(jnp.float32)
    total = first * first
    second = (rows[1][:, None] - cols[1][None, :]).astype(jnp.float32)
    total = total + second * second
    third = (rows[2][:, None] - cols[2][None, :]).astype(jnp.float32)
    total = total + third * third
    return 0.25 * jnp.exp(-jnp.sqrt(total) / 6.4)


def shards(row_cells, col_cells, omega):
    rank = omega.shape[0]
    local_rows = row_cells.shape[1]
    local_cols = col_cells.shape[1]
    rows_total = local_rows * lax.axis_size("row")
    order = local_cols * lax.axis_size("col")
    width = min(local_cols, 2048)
    count = local_cols // width

    def tile_at(index):
        cols = lax.dynamic_slice_in_dim(col_cells, index * width, width, 1)
        return kernel_tile(row_cells, cols)

    tiles = lax.map(tile_at, jnp.arange(count, dtype=jnp.int32))
    sketch_part = jnp.einsum(
        "kbw,bmw->km", omega.reshape(rank, count, width), tiles, precision=lax.Precision.HIGHEST
    )
    sketch = lax.psum(sketch_part, "col")
    gram = lax.psum(jnp.dot(sketch, sketch.T, precision=lax.Precision.HIGHEST), "row") / rows_total
    lower = jnp.linalg.cholesky(gram)
    basis = jax.scipy.linalg.solve_triangular(lower, sketch, lower=True)
    image_part = jnp.einsum("km,bmw->kbw", basis, tiles, precision=lax.Precision.HIGHEST).reshape(
        rank, local_cols
    )
    image = lax.psum(image_part, "row")
    core = lax.psum(jnp.dot(image, image.T, precision=lax.Precision.HIGHEST), "col") / order
    return (basis, image, core)


def solution(mesh):
    return jax.shard_map(
        shards,
        mesh=mesh,
        in_specs=(P(None, "row"), P(None, "col"), P(None, "col")),
        out_specs=(P(None, "row"), P(None, "col"), P()),
        check_vma=False,
    )
```

profile of v0, /device:TPU:0, one launch (start us, length us, event | category | flops | bytes accessed | tf_op | source)
XLA Modules:
  0.0 236.3 jit_solution(15518683551914293562)
XLA Ops:
  7.2 0.0 all-reduce.3.cloned.1.call-start
  7.2 0.0 copy-start
  7.2 43.4 %while.10 = (s32[]{:T(128)}, f32[4,1024,2048]{2,1,0:T(8,128)}, s32[3,1024]{1,0:T(4,128)}, s32[4]{0:T(128)S(1)}, s32[3,8192]{1,0:T(4,128)}, /*index=5*/s32[]{:T(1...) while((s32[]{:T(128)}, f32[4,1024,2048]{2,1,0:T(8,128)}, s32[3,1024]{1,0:T(4,128)}, ...), condition=%wide.region_1.2_spmd, body=%wide.region_0.1_spmd.sunk | while | flops 29360136 | bytes 8499915 | solution.py:30
  7.3 0.6 dynamic_slice.8
  8.5 1.0 constant_dynamic-slice_fusion.2
  9.5 0.8 fusion.18
  10.3 7.8 %multiply_dynamic-update-slice_fusion.2 = f32[4,1024,2048]{2,1,0:T(8,128)} fusion(f32[4,1024,2048]{2,1,0:T(8,128)} %get-tuple-element.102, s32[]{:T(128)} %get-tuple-element.101, s32[2048]{0:T(1024)S(1)} %bitcast.54, s32[1024]{0:T(1024)S(1)} %bitcast.57, s32[2048]{0:T(1024)S(1)} %bitcast.53, s32[1024]{0:T(1024)S(1)} %bitcast.58, s32[2048]{0:T(1024)S(1)} %bitcast.52, ...), kind=kLoop, calls=%fused_computation.clone.1 | loop fusion | flops 29360128 | bytes 8425984 | tf_op jit(solution)/shard_map/while/body/jit(dynamic_update_index_in_dim)/dynamic_update_slice | solution.py:30
  18.1 0.6 dynamic_slice.8
  19.4 1.0 constant_dynamic-slice_fusion.2
  20.3 0.8 fusion.18
  21.2 7.8 %multiply_dynamic-update-slice_fusion.2 = f32[4,1024,2048]{2,1,0:T(8,128)} fusion(f32[4,1024,2048]{2,1,0:T(8,128)} %get-tuple-element.102, s32[]{:T(128)} %get-tuple-element.101, s32[2048]{0:T(1024)S(1)} %bitcast.54, s32[1024]{0:T(1024)S(1)} %bitcast.57, s32[2048]{0:T(1024)S(1)} %bitcast.53, s32[1024]{0:T(1024)S(1)} %bitcast.58, s32[2048]{0:T(1024)S(1)} %bitcast.52, ...), kind=kLoop, calls=%fused_computation.clone.1 | loop fusion | flops 29360128 | bytes 8425984 | tf_op jit(solution)/shard_map/while/body/jit(dynamic_update_index_in_dim)/dynamic_update_slice | solution.py:30
  29.0 0.6 dynamic_slice.8
  30.2 1.0 constant_dynamic-slice_fusion.2
  31.2 0.8 fusion.18
  32.0 7.8 %multiply_dynamic-update-slice_fusion.2 = f32[4,1024,2048]{2,1,0:T(8,128)} fusion(f32[4,1024,2048]{2,1,0:T(8,128)} %get-tuple-element.102, s32[]{:T(128)} %get-tuple-element.101, s32[2048]{0:T(1024)S(1)} %bitcast.54, s32[1024]{0:T(1024)S(1)} %bitcast.57, s32[2048]{0:T(1024)S(1)} %bitcast.53, s32[1024]{0:T(1024)S(1)} %bitcast.58, s32[2048]{0:T(1024)S(1)} %bitcast.52, ...), kind=kLoop, calls=%fused_computation.clone.1 | loop fusion | flops 29360128 | bytes 8425984 | tf_op jit(solution)/shard_map/while/body/jit(dynamic_update_index_in_dim)/dynamic_update_slice | solution.py:30
  39.8 0.6 dynamic_slice.8
  41.1 1.0 constant_dynamic-slice_fusion.2
  42.0 0.8 fusion.18
  42.9 7.8 %multiply_dynamic-update-slice_fusion.2 = f32[4,1024,2048]{2,1,0:T(8,128)} fusion(f32[4,1024,2048]{2,1,0:T(8,128)} %get-tuple-element.102, s32[]{:T(128)} %get-tuple-element.101, s32[2048]{0:T(1024)S(1)} %bitcast.54, s32[1024]{0:T(1024)S(1)} %bitcast.57, s32[2048]{0:T(1024)S(1)} %bitcast.53, s32[1024]{0:T(1024)S(1)} %bitcast.58, s32[2048]{0:T(1024)S(1)} %bitcast.52, ...), kind=kLoop, calls=%fused_computation.clone.1 | loop fusion | flops 29360128 | bytes 8425984 | tf_op jit(solution)/shard_map/while/body/jit(dynamic_update_index_in_dim)/dynamic_update_slice | solution.py:30
  50.6 0.0 copy-done
  50.7 32.5 %convolution_bitcast_fusion.1 = f32[16,1024]{1,0:T(8,128)} fusion(f32[4,1024,2048]{2,1,0:T(8,128)} %get-tuple-element.30, f32[2,4,8,2048]{3,2,1,0:T(8,128)S(1)} %bitcast.55), kind=kOutput, calls=%fused_computation.3 | convolution fusion | flops 1610612736 | bytes 34144256 | tf_op jit(solution)/shard_map/kbw,bmw->km/dot_general | solution.py:31
  83.2 0.0 all-reduce.3.cloned.1.call-update
  83.2 0.0 all-reduce.5.cloned.1.call-start
  83.2 37.1 %all-reduce.3.cloned.1.call-done = f32[16,1024]{1,0:T(8,128)} async-done(((f32[16,1024]{1,0:T(8,128)}), f32[16,1024]{1,0:T(8,128)}) %all-reduce.3.cloned.1.call-update) | async-done | bytes 65552 | tf_op jit(solution)/shard_map/psum | solution.py:34
  120.4 1.1 fusion.8
  121.4 12.3 %psum.29 = f32[16,16]{0,1:T(8,128)S(1)} all-reduce(f32[16,16]{0,1:T(8,128)S(1)} %fusion.8), channel_id=1, replica_groups=mesh['row'=8,'col'=4] {'row'}, use_global_device_ids=true, to_apply=%region_3.4 | all-reduce | flops 256 | bytes 2048 | tf_op jit(solution)/shard_map/psum | solution.py:35
  133.8 0.1 copy.11
  133.9 1.5 cholesky.16
  135.4 0.6 compare_reduce_fusion
  136.0 0.6 fusion.3
  136.7 1.2 custom-call.7
  137.9 1.1 fusion.4
  139.0 0.0 copy-start.1
  139.0 19.6 %convolution_bitcast_fusion = f32[4,2,8,2048]{3,2,1,0:T(8,128)S(1)} fusion(f32[4,1024,2048]{2,1,0:T(8,128)} %get-tuple-element.30, f32[16,1024]{1,0:T(8,128)S(1)} %fusion.4), kind=kOutput, calls=%fused_computation.2 | convolution fusion | flops 1610612736 | bytes 34144256 | tf_op jit(solution)/shard_map/km,bmw->kbw/dot_general | solution.py:38
  158.6 0.0 copy-done.1
  158.6 0.8 copy.15
  159.4 0.0 all-reduce.5.cloned.1.call-update
  159.5 53.8 %all-reduce.5.cloned.1.call-done = f32[16,8192]{1,0:T(8,128)} async-done(((f32[16,8192]{1,0:T(8,128)}), f32[16,8192]{1,0:T(8,128)}) %all-reduce.5.cloned.1.call-update) | async-done | bytes 524304 | tf_op jit(solution)/shard_map/psum | solution.py:41
  213.2 1.9 fusion.9
  215.2 11.8 %psum.31 = f32[16,16]{1,0:T(8,128)S(1)} all-reduce(f32[16,16]{1,0:T(8,128)S(1)} %fusion.9), channel_id=1, replica_groups=mesh['row'=8,'col'=4] {'col'}, use_global_device_ids=true, to_apply=%region_7.8 | all-reduce | flops 256 | bytes 2048 | tf_op jit(solution)/shard_map/psum | solution.py:42
  227.0 0.6 broadcast_multiply_fusion
  227.6 1.9 copy.29
  (5 shorter events, 0.0 us)
Async XLA Ops:
  7.2 113.2 %all-reduce.3.cloned.1.call-start = ((), (), s32[]{:S(2)}) async-start(), calls=%async_computation | async-start | bytes 131072 | tf_op jit(solution)/shard_map/psum | solution.py:34
  7.2 43.4 %copy-start = (f32[16,8192]{1,0:T(8,128)S(1)}, f32[16,8192]{1,0:T(8,128)}, u32[]{:S(2)}) copy-start(f32[16,8192]{1,0:T(8,128)} %param.7) | copy-start | bytes 1572868
  83.2 130.0 %all-reduce.5.cloned.1.call-start = ((), (), s32[]{:S(2)}) async-start(), calls=%async_computation.1 | async-start | bytes 1048576 | tf_op jit(solution)/shard_map/psum | solution.py:41
  139.0 19.6 %copy-start.1 = (f32[16,1024]{1,0:T(8,128)}, f32[16,1024]{1,0:T(8,128)S(1)}, u32[]{:S(2)}) copy-start(f32[16,1024]{1,0:T(8,128)S(1)} %fusion.4) | copy-start | bytes 196612
Sparse Core Ops, SparseCore 0:
  83.3 37.0 all-reduce.2
  159.6 53.5 all-reduce.4
where the time goes:
time: 237 us; the launch traced here: 236 us
  waiting for transfers between devices  90.9 us (38%)
  matrix products  56.2 us (24%)
  other arithmetic  35.7 us (15%)
  blocking collectives  24.1 us (10%)
  between operations  14.1 us (6%)
  local copies, waits for them, and re-layouts  12.4 us (5%)
  loops' own time  2.68 us (1%)
    psum x1, waiting for transfers between devices, shards(): image = lax.psum(image_part, 'row')  53.8 us
    psum x1, waiting for transfers between devices, shards(): sketch = lax.psum(sketch_part, 'col')  37.1 us
    dot_general x1, matrix products, shards(): jnp.einsum('kbw,bmw->km', omega.reshape(rank, count, width), tiles, preci...  32.5 us
    dynamic_update_slice x4, other arithmetic, shards(): tiles = lax.map(tile_at, jnp.arange(count, dtype=jnp.int32))  31.1 us
    dot_general x1, matrix products, shards(): jnp.einsum('km,bmw->kbw', basis, tiles, precision=lax.Precision.HIGHEST)  19.6 us
    psum x1, blocking collectives, shards(): lax.psum(jnp.dot(sketch, sketch.T, precision=lax.Precision.HIGHEST), 'row')  12.3 us
    psum x1, blocking collectives, shards(): lax.psum(jnp.dot(image, image.T, precision=lax.Precision.HIGHEST), 'col')  11.8 us
    slice x8, local copies, waits for them, and re-layouts, kernel_tile(): first = (rows[0][:, None] - cols[0][None, :]).astype(jnp.float32)  7.27 us
  transfers between devices with their start and end apart: 2, of which 2 were waited for; matrix products, arithmetic and copies ran while one was open for 0% of the time, Pallas kernels for 0%

commit v1 on v0

v1 whole, which is shorter than its diff:
```python
import functools
import math

import jax
import jax.numpy as jnp
from jax import lax
from jax.experimental import pallas as pl
from jax.experimental.pallas import tpu as pltpu
from jax.sharding import PartitionSpec as P

BF16, F32 = jnp.bfloat16, jnp.float32
HIGHEST = lax.Precision.HIGHEST
NT = (((1,), (1,)), ((), ()))
NN = (((1,), (0,)), ((), ()))
FEATS = 128
RATE = -math.log2(math.e) / 6.4


def split(x):
    high = x.astype(BF16)
    return high, (x - high.astype(F32)).astype(BF16)


def features(cells, extent, own):
    c0, c1, c2 = (cells[d : d + 1, :].astype(F32) for d in range(3))
    norm = c0 * c0 + c1 * c1 + c2 * c2
    top = jnp.floor(norm * (1.0 / 128.0)) * 128.0
    rest = norm - top
    one = jnp.ones_like(norm)
    if own:
        rows = [c0, c1, c2, top, rest, one, one]
    else:
        rows = [-2.0 * c0, -2.0 * c1, -2.0 * c2, one, one, top, rest]
    at = lax.broadcasted_iota(jnp.int32, (extent, norm.shape[1]), 0)
    out = jnp.zeros((extent, norm.shape[1]), F32)
    for index, row in enumerate(rows):
        out = jnp.where(at == index, row, out)
    return out


def kernel(
    shape,
    row_ref, col_ref, omega_ref,
    basis_ref, image_ref, core_ref,
    rowf, colf, om, khi, klo,
    sk_src, sk_all, sk_hl, g_src, g_all, w_src, w_all, img, c_src, c_all, d_src, d_all,
    sk_ss, sk_rs, g_ss, g_rs, w_ss, w_rs, a_ss, a_rs, f_ss, f_rs, c_ss, c_rs, d_ss, d_rs,
):
    R, C, rank, M, N, chunk, wide, rows_total, order = shape
    me = lax.axis_index("row")
    mc = lax.axis_index("col")
    half = R // 2
    sib = me + 1 - 2 * lax.rem(me, 2)
    part = N // R
    chunks = M // chunk

    def row_of(t):
        return lax.rem(me + t, R)

    def row_from(t):
        return lax.rem(me - t + R, R)

    def remote(src, dst, ss, rs, axis, peer):
        return pltpu.make_async_remote_copy(
            src_ref=src, dst_ref=dst, send_sem=ss, recv_sem=rs,
            device_id={axis: peer}, device_id_type=pl.DeviceIdType.MESH,
        )

    barrier = pltpu.get_barrier_semaphore()
    for t in range(1, R):
        pl.semaphore_signal(barrier, inc=1, device_id={"row": row_of(t)}, device_id_type=pl.DeviceIdType.MESH)
    for t in range(1, C):
        pl.semaphore_signal(
            barrier, inc=1, device_id={"col": lax.rem(mc + t, C)}, device_id_type=pl.DeviceIdType.MESH
        )

    rowf[...] = features(row_ref, FEATS, True).T.astype(BF16)
    step = min(N, 1024)
    for s in range(N // step):
        cols = pl.ds(s * step, step)
        colf[:, cols] = features(col_ref.at[:, cols], FEATS, False).astype(BF16)
        high, low = split(0.25 * omega_ref[:, cols])
        om[0:rank, cols] = high
        om[rank : 2 * rank, cols] = low

    pl.semaphore_wait(barrier, R - 1 + C - 1)

    def sketch_copy(rc, t):
        return remote(
            sk_src.at[rc], sk_all.at[mc, rc], sk_ss.at[rc, t], sk_rs.at[rc, t], "col", lax.rem(mc + t, C)
        )

    def row_chunk(rc, carry):
        rows = pl.ds(pl.multiple_of(rc * chunk, chunk), chunk)

        def col_tile(ct, acc):
            cols = pl.ds(pl.multiple_of(ct * wide, wide), wide)
            sq = lax.dot_general(rowf[rows, :], colf[:, cols], NN, preferred_element_type=F32)
            sq = jnp.maximum(sq, 1e-30)
            value = jnp.exp2((sq * RATE) * lax.rsqrt(sq))
            high, low = split(value)
            khi[rows, cols] = high
            klo[rows, cols] = low
            o = om[:, cols]
            return (
                acc
                + lax.dot_general(o, high, NT, preferred_element_type=F32)
                + lax.dot_general(o, low, NT, preferred_element_type=F32)
            )

        acc = lax.fori_loop(0, N // wide, col_tile, jnp.zeros((2 * rank, chunk), F32))
        total = acc[:rank] + acc[rank:]
        sk_src[rc] = total
        sk_all[mc, rc] = total
        for t in range(1, C):
            sketch_copy(rc, t).start()
        return carry

    lax.fori_loop(0, chunks, row_chunk, 0)

    for rc in range(chunks):
        for t in range(1, C):
            sketch_copy(rc, t).wait_recv()
    pieces = []
    for rc in range(chunks):
        total = sk_all[0, rc]
        for c in range(1, C):
            total = total + sk_all[c, rc]
        pieces.append(total)
    sketch = jnp.concatenate(pieces, axis=1)
    high, low = split(0.25 * sketch)
    sk_hl[0:rank, :] = high
    sk_hl[rank : 2 * rank, :] = low
    gram = lax.dot_general(sketch, sketch, NT, precision=HIGHEST, preferred_element_type=F32) / rows_total
    g_src[...] = jnp.zeros_like(g_src)
    g_src[:, rank : 2 * rank] = gram
    g_all[me] = g_src[...]

    def gram_copy(t):
        return remote(g_src, g_all.at[me], g_ss.at[t], g_rs.at[t], "row", row_of(t))

    for t in range(1, R):
        gram_copy(t).start()

    def w_copy(t):
        return remote(w_src.at[t], w_all.at[me], w_ss.at[t], w_rs.at[t], "row", row_of(t))

    def product(peer):
        cols = pl.ds(pl.multiple_of(peer * part, part), part)
        s = sk_hl[...]
        acc = lax.dot_general(s, khi[:, cols], NN, preferred_element_type=F32)
        acc = acc + lax.dot_general(s, klo[:, cols], NN, preferred_element_type=F32)
        return acc[:rank] + acc[rank:]

    def block(t, carry):
        w_src[t] = product(row_of(t))
        w_copy(t).start()
        return carry

    lax.fori_loop(1, R, block, 0)
    w_all[me] = product(me)

    for t in range(1, R):
        gram_copy(t).wait_recv()
    mat = g_all[0]
    for r in range(1, R):
        mat = mat + g_all[r]
    sub = lax.broadcasted_iota(jnp.int32, mat.shape, 0)
    lane = lax.broadcasted_iota(jnp.int32, mat.shape, 1)
    mat = mat + jnp.where(lane == sub, 1.0, 0.0)
    for k in range(rank - 1):
        row = mat[k : k + 1, :]
        factor = mat[:, rank + k : rank + k + 1] * (1.0 / mat[k : k + 1, rank + k : rank + k + 1])
        mat = mat - jnp.where(sub > k, factor * row, 0.0)
    diag = jnp.sum(jnp.where(lane == sub + rank, mat, 0.0), axis=1, keepdims=True)
    inverse = (mat * (1.0 / jnp.sqrt(diag)))[:, :rank]
    inverse = jnp.where(lane[:, :rank] <= sub[:, :rank], inverse, 0.0)
    basis_ref[...] = jnp.dot(inverse, sketch, precision=HIGHEST, preferred_element_type=F32)

    for t in range(1, R):
        w_copy(t).wait_recv()
    total = w_all[0]
    for r in range(1, R):
        total = total + w_all[r]
    mine = jnp.dot(inverse, total, precision=HIGHEST, preferred_element_type=F32)
    img[me] = mine

    def far_copy(t):
        return remote(img.at[me], img.at[me], a_ss.at[t], a_rs.at[t], "row", row_of(2 * t))

    def near_copy(t):
        slot = row_from(2 * t)
        return remote(img.at[slot], img.at[slot], f_ss.at[t], f_rs.at[t], "row", sib)

    def core_copy(t):
        return remote(c_src, c_all.at[me], c_ss.at[t], c_rs.at[t], "row", row_of(t))

    def last_copy(t):
        return remote(d_src, d_all.at[mc], d_ss.at[t], d_rs.at[t], "col", lax.rem(mc + t, C))

    core = lax.dot_general(mine, mine, NT, precision=HIGHEST, preferred_element_type=F32) / order
    c_src[...] = jnp.zeros_like(c_src)
    c_src[:, 0:rank] = core
    c_all[me] = c_src[...]
    for t in range(1, R):
        core_copy(t).start()
    for t in range(half - 1, 0, -1):
        far_copy(t).start()
    near_copy(0).start()
    for t in range(1, R):
        core_copy(t).wait_recv()
    core = c_all[0]
    for r in range(1, R):
        core = core + c_all[r]
    d_src[...] = core
    d_all[mc] = core
    for t in range(1, C):
        last_copy(t).start()
    for t in range(1, half):
        far_copy(t).wait_recv()
        near_copy(t).start()
    for t in range(half):
        near_copy(t).wait_recv()
    for r in range(R):
        image_ref[:, r * part : (r + 1) * part] = img[r]
    for t in range(1, C):
        last_copy(t).wait_recv()
    core = d_all[0]
    for c in range(1, C):
        core = core + d_all[c]
    core_ref[...] = core[:, 0:rank]

    for rc in range(chunks):
        for t in range(1, C):
            sketch_copy(rc, t).wait_send()
    for t in range(1, R):
        gram_copy(t).wait_send()
        w_copy(t).wait_send()
        core_copy(t).wait_send()
    for t in range(1, half):
        far_copy(t).wait_send()
    for t in range(half):
        near_copy(t).wait_send()
    for t in range(1, C):
        last_copy(t).wait_send()


def shards(row_cells, col_cells, omega):
    R, C = lax.axis_size("row"), lax.axis_size("col")
    rank = omega.shape[0]
    M, N = row_cells.shape[1], col_cells.shape[1]
    chunk, wide = min(M, 256), min(N, 1024)
    chunks, part = M // chunk, N // R
    shape = (R, C, rank, M, N, chunk, wide, M * R, N * C)
    lanes = 128
    vmem = pltpu.VMEM
    dma = pltpu.SemaphoreType.DMA
    full = pl.BlockSpec(memory_space=pltpu.VMEM)
    return pl.pallas_call(
        functools.partial(kernel, shape),
        out_shape=(
            jax.ShapeDtypeStruct((rank, M), F32),
            jax.ShapeDtypeStruct((rank, N), F32),
            jax.ShapeDtypeStruct((rank, rank), F32),
        ),
        in_specs=[full] * 3,
        out_specs=(full,) * 3,
        scratch_shapes=[
            vmem((M, FEATS), BF16),
            vmem((FEATS, N), BF16),
            vmem((2 * rank, N), BF16),
            vmem((M, N), BF16),
            vmem((M, N), BF16),
            vmem((chunks, rank, chunk), F32),
            vmem((C, chunks, rank, chunk), F32),
            vmem((2 * rank, M), BF16),
            vmem((rank, lanes), F32),
            vmem((R, rank, lanes), F32),
            vmem((R, rank, part), F32),
            vmem((R, rank, part), F32),
            vmem((R, rank, part), F32),
            vmem((rank, lanes), F32),
            vmem((R, rank, lanes), F32),
            vmem((rank, lanes), F32),
            vmem((C, rank, lanes), F32),
            dma((chunks, C)), dma((chunks, C)),
            dma((R,)), dma((R,)),
            dma((R,)), dma((R,)),
            dma((R,)), dma((R,)),
            dma((R,)), dma((R,)),
            dma((R,)), dma((R,)),
            dma((C,)), dma((C,)),
        ],
        compiler_params=pltpu.CompilerParams(
            collective_id=0, has_side_effects=True, vmem_limit_bytes=60 * 1024 * 1024
        ),
    )(row_cells, col_cells, omega)


def solution(mesh):
    return jax.shard_map(
        shards,
        mesh=mesh,
        in_specs=(P(None, "row"), P(None, "col"), P(None, "col")),
        out_specs=(P(None, "row"), P(None, "col"), P()),
        check_vma=False,
    )
```

time: 237 us -> 58.5 us (0.25)
  waiting for transfers between devices: 90.9 us -> 0 us
  matrix products: 56.2 us -> 0 us
  Pallas kernels: 0 us -> 53.7 us
  other arithmetic: 35.7 us -> 0 us
  blocking collectives: 24.1 us -> 0 us
  between operations: 14.1 us -> 0.64 us
  local copies, waits for them, and re-layouts: 12.4 us -> 3.96 us
  loops' own time: 2.68 us -> 0 us
    psum x2 -> x0, waiting for transfers between devices: 90.9 us -> none  [the longest x1 53.8 us: shards(): image = lax.psum(image_part, 'row')]
    dot_general x4 -> x0, matrix products: 55.1 us -> none  [the longest x1 32.5 us: shards(): jnp.einsum('kbw,bmw->km', omega.reshape(rank, count, width), tiles, preci...]
    pallas_call x0 -> x1, Pallas kernels: none -> 53.7 us  [shards(): pl.pallas_call(functools.partial(kernel, shape), out_shape=(jax.ShapeDtyp...]
    dynamic_update_slice x4 -> x0, other arithmetic: 31.1 us -> none  [shards(): tiles = lax.map(tile_at, jnp.arange(count, dtype=jnp.int32))]
    psum x2 -> x0, blocking collectives: 24.1 us -> none  [the longest x1 12.3 us: shards(): lax.psum(jnp.dot(sketch, sketch.T, precision=lax.Precision.HIGHEST), 'row')]
    slice x8 -> x0, local copies, waits for them, and re-layouts: 7.27 us -> none  [kernel_tile(): first = (rows[0][:, None] - cols[0][None, :]).astype(jnp.float32)]
    another operation x5 -> x0, other arithmetic: 4.01 us -> none  [the longest x3 2.13 us: shards(): lower = jnp.linalg.cholesky(gram)]
    another operation x1 -> x0, loops' own time: 2.68 us -> none  [shards(): tiles = lax.map(tile_at, jnp.arange(count, dtype=jnp.int32))]
  transfers between devices with their start and end apart: 2 -> 0, of which waited for: 2 -> 0; matrix products, arithmetic and copies ran while one was open for 0% -> 0% of each run, Pallas kernels for 0% -> 0%
where the time goes in v1:
time: 58.5 us; the launch traced here: 58.3 us
  Pallas kernels  53.7 us (92%)
  local copies, waits for them, and re-layouts  3.96 us (7%)
  between operations  0.64 us (1%)
    pallas_call x1, Pallas kernels, shards(): pl.pallas_call(functools.partial(kernel, shape), out_shape=(jax.ShapeDtyp...  53.7 us
    unnamed x5, local copies, waits for them, and re-layouts  3.96 us

profile of v1, /device:TPU:0, one launch (start us, length us, event | category | flops | bytes accessed | tf_op | source)
XLA Modules:
  0.0 58.3 jit_solution(1537569052709850789)
XLA Ops:
  0.6 53.7 %shard_map.58 = (f32[16,1024]{1,0:T(8,128)}, f32[16,8192]{1,0:T(8,128)}, f32[16,16]{1,0:T(8,128)}) custom-call(s32[3,1024]{1,0:T(4,128)} %row_ref.1, s32[3,8192]{1,0:T(4,128)} %col_ref.1, f32[16,8192]{1,0:T(8,128)} %omega_ref.1), custom_call_target="tpu_custom_call" | custom-call | tf_op jit(solution)/shard_map/pallas_call | solution.py:259
  54.3 1.5 %copy.9 = f32[16,1024]{1,0:T(8,128)} copy(f32[16,1024]{1,0:T(8,128)} %get-tuple-element.6) | data formatting | bytes 131072
  55.8 0.0 copy-start
  55.8 1.9 %copy.10 = f32[16,8192]{1,0:T(8,128)} copy(f32[16,8192]{1,0:T(8,128)} %get-tuple-element.7) | data formatting | bytes 1048576
  57.7 0.0 copy-done
  57.7 0.6 %copy.11 = f32[16,16]{1,0:T(8,128)} copy(f32[16,16]{1,0:T(8,128)S(1)} %copy-done) | data formatting | bytes 2048
Async XLA Ops:
  55.8 1.9 %copy-start = (f32[16,16]{1,0:T(8,128)S(1)}, f32[16,16]{1,0:T(8,128)}, u32[]{:S(2)}) copy-start(f32[16,16]{1,0:T(8,128)} %get-tuple-element.8) | copy-start | bytes 3076

commit v2 on v1

--- a/solution.py
+++ b/solution.py
@@ -12,37 +12,20 @@
 HIGHEST = lax.Precision.HIGHEST
 NT = (((1,), (1,)), ((), ()))
 NN = (((1,), (0,)), ((), ()))
-FEATS = 128
+LANES = 128
 RATE = -math.log2(math.e) / 6.4
 
 
 def split(x):
     high = x.astype(BF16)
     return high, (x - high.astype(F32)).astype(BF16)
-
-
-def features(cells, extent, own):
-    c0, c1, c2 = (cells[d : d + 1, :].astype(F32) for d in range(3))
-    norm = c0 * c0 + c1 * c1 + c2 * c2
-    top = jnp.floor(norm * (1.0 / 128.0)) * 128.0
-    rest = norm - top
-    one = jnp.ones_like(norm)
-    if own:
-        rows = [c0, c1, c2, top, rest, one, one]
-    else:
-        rows = [-2.0 * c0, -2.0 * c1, -2.0 * c2, one, one, top, rest]
-    at = lax.broadcasted_iota(jnp.int32, (extent, norm.shape[1]), 0)
-    out = jnp.zeros((extent, norm.shape[1]), F32)
-    for index, row in enumerate(rows):
-        out = jnp.where(at == index, row, out)
-    return out
 
 
 def kernel(
     shape,
     row_ref, col_ref, omega_ref,
     basis_ref, image_ref, core_ref,
-    rowf, colf, om, khi, klo,
+    rowb, colc, om, khi, klo,
     sk_src, sk_all, sk_hl, g_src, g_all, w_src, w_all, img, c_src, c_all, d_src, d_all,
     sk_ss, sk_rs, g_ss, g_rs, w_ss, w_rs, a_ss, a_rs, f_ss, f_rs, c_ss, c_rs, d_ss, d_rs,
 ):
@@ -74,11 +57,12 @@
             barrier, inc=1, device_id={"col": lax.rem(mc + t, C)}, device_id_type=pl.DeviceIdType.MESH
         )
 
-    rowf[...] = features(row_ref, FEATS, True).T.astype(BF16)
+    for d in range(3):
+        rowb[d] = jnp.broadcast_to(row_ref[d : d + 1, :].astype(F32), (LANES, M)).T
     step = min(N, 1024)
     for s in range(N // step):
         cols = pl.ds(s * step, step)
-        colf[:, cols] = features(col_ref.at[:, cols], FEATS, False).astype(BF16)
+        colc[0:3, cols] = col_ref[:, cols].astype(F32)
         high, low = split(0.25 * omega_ref[:, cols])
         om[0:rank, cols] = high
         om[rank : 2 * rank, cols] = low
@@ -95,7 +79,11 @@
 
         def col_tile(ct, acc):
             cols = pl.ds(pl.multiple_of(ct * wide, wide), wide)
-            sq = lax.dot_general(rowf[rows, :], colf[:, cols], NN, preferred_element_type=F32)
+            repeat = (1, wide // LANES)
+            sq = None
+            for d in range(3):
+                gap = jnp.tile(rowb[d, rows, :], repeat) - colc[d : d + 1, cols]
+                sq = gap * gap if sq is None else sq + gap * gap
             sq = jnp.maximum(sq, 1e-30)
             value = jnp.exp2((sq * RATE) * lax.rsqrt(sq))
             high, low = split(value)
@@ -245,6 +233,11 @@
         last_copy(t).wait_send()
 
 
+def finish(*refs):
+    for source, target in zip(refs[:3], refs[3:]):
+        target[...] = source[...]
+
+
 def shards(row_cells, col_cells, omega):
     R, C = lax.axis_size("row"), lax.axis_size("col")
     rank = omega.shape[0]
@@ -252,37 +245,37 @@
     chunk, wide = min(M, 256), min(N, 1024)
     chunks, part = M // chunk, N // R
     shape = (R, C, rank, M, N, chunk, wide, M * R, N * C)
-    lanes = 128
     vmem = pltpu.VMEM
     dma = pltpu.SemaphoreType.DMA
     full = pl.BlockSpec(memory_space=pltpu.VMEM)
-    return pl.pallas_call(
+    out_shape = (
+        jax.ShapeDtypeStruct((rank, M), F32),
+        jax.ShapeDtypeStruct((rank, N), F32),
+        jax.ShapeDtypeStruct((rank, rank), F32),
+    )
+    outs = pl.pallas_call(
         functools.partial(kernel, shape),
-        out_shape=(
-            jax.ShapeDtypeStruct((rank, M), F32),
-            jax.ShapeDtypeStruct((rank, N), F32),
-            jax.ShapeDtypeStruct((rank, rank), F32),
-        ),
+        out_shape=out_shape,
         in_specs=[full] * 3,
         out_specs=(full,) * 3,
         scratch_shapes=[
-            vmem((M, FEATS), BF16),
-            vmem((FEATS, N), BF16),
+            vmem((3, M, LANES), F32),
+            vmem((8, N), F32),
             vmem((2 * rank, N), BF16),
             vmem((M, N), BF16),
             vmem((M, N), BF16),
             vmem((chunks, rank, chunk), F32),
             vmem((C, chunks, rank, chunk), F32),
             vmem((2 * rank, M), BF16),
-            vmem((rank, lanes), F32),
-            vmem((R, rank, lanes), F32),
+            vmem((rank, LANES), F32),
+            vmem((R, rank, LANES), F32),
             vmem((R, rank, part), F32),
             vmem((R, rank, part), F32),
             vmem((R, rank, part), F32),
-            vmem((rank, lanes), F32),
-            vmem((R, rank, lanes), F32),
-            vmem((rank, lanes), F32),
-            vmem((C, rank, lanes), F32),
+            vmem((rank, LANES), F32),
+            vmem((R, rank, LANES), F32),
+            vmem((rank, LANES), F32),
+            vmem((C, rank, LANES), F32),
             dma((chunks, C)), dma((chunks, C)),
             dma((R,)), dma((R,)),
             dma((R,)), dma((R,)),
@@ -292,9 +285,16 @@
             dma((C,)), dma((C,)),
         ],
         compiler_params=pltpu.CompilerParams(
-            collective_id=0, has_side_effects=True, vmem_limit_bytes=60 * 1024 * 1024
+            collective_id=0, has_side_effects=True, vmem_limit_bytes=46 * 1024 * 1024
         ),
     )(row_cells, col_cells, omega)
+    return pl.pallas_call(
+        finish,
+        out_shape=out_shape,
+        in_specs=[full] * 3,
+        out_specs=(full,) * 3,
+        compiler_params=pltpu.CompilerParams(vmem_limit_bytes=4 * 1024 * 1024),
+    )(*outs)
 
 
 def solution(mesh):

time: 58.5 us -> 54.6 us (0.933)
  Pallas kernels: 53.7 us -> 51.1 us
  local copies, waits for them, and re-layouts: 3.96 us -> 2.66 us
    pallas_call x1 -> x2, Pallas kernels: 53.7 us -> 51.1 us  [the longest x1 50.2 us: shards(): pl.pallas_call(functools.partial(kernel, shape), out_shape=out_shape, in_...]
    unnamed x5 -> x6, local copies, waits for them, and re-layouts: 3.96 us -> 2.66 us
where the time goes in v2:
time: 54.6 us; the launch traced here: 54.4 us
  Pallas kernels  51.1 us (94%)
  local copies, waits for them, and re-layouts  2.66 us (5%)
  between operations  0.65 us (1%)
    pallas_call x1, Pallas kernels, shards(): pl.pallas_call(functools.partial(kernel, shape), out_shape=out_shape, in_...  50.2 us
    unnamed x6, local copies, waits for them, and re-layouts  2.66 us

profile of v2, /device:TPU:0, one launch (start us, length us, event | category | flops | bytes accessed | tf_op | source)
XLA Modules:
  0.0 54.4 jit_solution(16260776731345281092)
XLA Ops:
  0.6 0.0 copy-start
  0.6 1.0 %copy-done = f32[16,8192]{1,0:T(8,128)S(1)} copy-done((f32[16,8192]{1,0:T(8,128)S(1)}, f32[16,8192]{1,0:T(8,128)}, u32[]{:S(2)}) %copy-start) | copy-done | bytes 524312
  1.7 0.0 copy-start.1
  1.7 0.9 %copy-done.1 = s32[3,8192]{1,0:T(4,128)S(1)} copy-done((s32[3,8192]{1,0:T(4,128)S(1)}, s32[3,8192]{1,0:T(4,128)}, u32[]{:S(2)}) %copy-start.1) | copy-done | bytes 98328
  2.6 0.0 copy-start.2
  2.6 0.7 %copy-done.2 = s32[3,1024]{1,0:T(4,128)S(1)} copy-done((s32[3,1024]{1,0:T(4,128)S(1)}, s32[3,1024]{1,0:T(4,128)}, u32[]{:S(2)}) %copy-start.2) | copy-done | bytes 12312
  3.3 50.2 %shard_map.58 = (f32[16,1024]{1,0:T(8,128)S(1)}, f32[16,8192]{1,0:T(8,128)S(1)}, f32[16,16]{1,0:T(8,128)S(1)}) custom-call(s32[3,1024]{1,0:T(4,128)S(1)} %copy-done.2, s32[3,8192]{1,0:T(4,128)S(1)} %copy-done.1, f32[16,8192]{1,0:T(8,128)S(1)} %copy-done), custom_call_target="tpu_custom_call" | custom-call | tf_op jit(solution)/shard_map/pallas_call | solution.py:256
  53.5 0.8 %shard_map.59 = (f32[16,1024]{1,0:T(8,128)}, f32[16,8192]{1,0:T(8,128)}, f32[16,16]{1,0:T(8,128)}) custom-call(f32[16,1024]{1,0:T(8,128)S(1)} %get-tuple-element.6.refs_0_, f32[16,8192]{1,0:T(8,128)S(1)} %get-tuple-element.7.refs_1_, f32[16,16]{1,0:T(8,128)S(1)} %get-tuple-element.8.refs_2_), custom_call_target="tpu_custom_call" | custom-call | tf_op jit(solution)/shard_map/pallas_call | solution.py:291
Async XLA Ops:
  0.6 1.0 %copy-start = (f32[16,8192]{1,0:T(8,128)S(1)}, f32[16,8192]{1,0:T(8,128)}, u32[]{:S(2)}) copy-start(f32[16,8192]{1,0:T(8,128)} %omega_ref.1) | copy-start | bytes 1572868
  1.7 0.9 %copy-start.1 = (s32[3,8192]{1,0:T(4,128)S(1)}, s32[3,8192]{1,0:T(4,128)}, u32[]{:S(2)}) copy-start(s32[3,8192]{1,0:T(4,128)} %col_ref.1) | copy-start | bytes 294916
  2.6 0.7 %copy-start.2 = (s32[3,1024]{1,0:T(4,128)S(1)}, s32[3,1024]{1,0:T(4,128)}, u32[]{:S(2)}) copy-start(s32[3,1024]{1,0:T(4,128)} %row_ref.1) | copy-start | bytes 36868
